TPU v7x, 256 devices: a whole 4x4x8 slice. The times are simulated.
256 devices in a mesh: gx: 16 (over y_hi, x, core), gy: 16 (over y_lo, z).
Axes of the slice: x: 4, y: 4 (y_hi: 2, y_lo: 2; y = y_hi * 2 + y_lo), z: 8, core: 2. Of those that a mesh axis runs over, the one named last changes fastest.
Arguments:
- right_side: float32 [3, 256, 128, 256], P(None, 'gx', 'gy'), may hold values from -12 to 12
- labels: int32 [256, 128, 256], P('gx', 'gy'), may hold values 0 or 1
Outputs:
- solution: float32 [3, 256, 128, 256], P(None, 'gx', 'gy')
- residual: float32 [3, 256, 128, 256], P(None, 'gx', 'gy')
All inputs are finite; a program needn't handle non-finite values. No bound on the sum of `labels` on one device may be relied on, other than what follows from the above.
Results may differ from a plain program's by a relative error of at most 0.0003.
Values sent between devices are 32-bit elements; how exact they have to be, the bound alone decides.
A program may use at most 64 MiB of HBM per device.

v0:
```python
import jax
import jax.numpy as jnp
from jax import lax
from jax.experimental import pallas as pl
from jax.experimental.pallas import tpu as pltpu
from jax.sharding import PartitionSpec as P

MESH = pl.DeviceIdType.MESH
ITERS = 4
LAMBDA_SOFT = 0.5769231
LAMBDA_RISE = 1.6452991
SHEAR_SOFT = 0.3846154
SHEAR_RISE = 2.9487179
KAPPA = 0.05

NX, NY, NZ = 16, 8, 256
HALO = 4
PX = NX + 2 * HALO
PY = 16
GROUP = 16
SIGMA = 1.05
RAW = 16.0
STEP = 2.0 / (RAW * SIGMA)

DIRECTIONS = [(1, 0), (1, 1), (1, -1), (0, 1), (0, -1), (-1, 0), (-1, 1), (-1, -1)]
DOTS = [(0, 0), (0, 1), (1, 1), (1, 2), (2, 2), (2, 3), (3, 3), (3, 4)]


def phases(form):
    soft = form(LAMBDA_SOFT, SHEAR_SOFT)
    stiff = form(LAMBDA_SOFT + LAMBDA_RISE, SHEAR_SOFT + SHEAR_RISE)
    return soft, stiff


def pick(stiff_mask, form):
    soft, stiff = phases(form)
    return jnp.where(stiff_mask, jnp.float32(stiff), jnp.float32(soft))


def plane_modes(w_ref, plane, modes):
    for c in range(3):
        u = w_ref[c, plane]
        uz = pltpu.roll(u, NZ - 1, 1)
        s, d = u + uz, uz - u
        sy, dy = pltpu.roll(s, PY - 1, 0), pltpu.roll(d, PY - 1, 0)
        modes[4 * c] = s + sy
        modes[4 * c + 1] = sy - s
        modes[4 * c + 2] = d + dy
        modes[4 * c + 3] = dy - d


def voxel_forces(plane, label_ref, lower, upper, carry, total):
    for row in (0, 8):
        for lane in (0, 128):
            at = (slice(row, row + 8), slice(lane, lane + 128))
            stiff = label_ref[plane, at[0], at[1]] > 0
            lam = pick(stiff, lambda la, mu: la)
            mu = pick(stiff, lambda la, mu: mu)
            mu2 = pick(stiff, lambda la, mu: 2.0 * mu)
            lam3 = pick(stiff, lambda la, mu: la / 3.0)
            mu3 = pick(stiff, lambda la, mu: mu / 3.0)
            dd9 = pick(stiff, lambda la, mu: (la + 4.0 * mu) / 9.0)
            a = [lower[i, at[0], at[1]] for i in range(12)]
            b = [upper[i, at[0], at[1]] for i in range(12)]
            d = [[b[4 * c + m] - a[4 * c + m] for m in range(4)] for c in range(3)]
            s = [[a[4 * c + m] + b[4 * c + m] if m else None for m in range(4)] for c in range(3)]
            fd = [[None] * 4 for _ in range(3)]
            fs = [[None] * 4 for _ in range(3)]
            trace = lam * (d[0][0] + s[1][1] + s[2][2])
            fd[0][0] = trace + mu2 * d[0][0]
            fs[1][1] = trace + mu2 * s[1][1]
            fs[2][2] = trace + mu2 * s[2][2]
            fd[1][0] = fs[0][1] = mu * (d[1][0] + s[0][1])
            fd[2][0] = fs[0][2] = mu * (d[2][0] + s[0][2])
            fs[2][1] = fs[1][2] = mu * (s[2][1] + s[1][2])
            h = lam3 * (d[0][1] + s[2][3])
            fd[0][1], fs[2][3] = h + mu * d[0][1], h + mu * s[2][3]
            h = lam3 * (d[0][2] + s[1][3])
            fd[0][2], fs[1][3] = h + mu * d[0][2], h + mu * s[1][3]
            h = lam3 * (d[1][1] + d[2][2])
            fd[1][1], fd[2][2] = h + mu * d[1][1], h + mu * d[2][2]
            three = s[0][3] + d[1][2] + d[2][1]
            fs[0][3] = mu3 * (s[0][3] + three)
            fd[1][2] = mu3 * (d[1][2] + three)
            fd[2][1] = mu3 * (d[2][1] + three)
            for c in range(3):
                fd[c][3] = dd9 * d[c][3]
            for c in range(3):
                for m in range(4):
                    i = 4 * c + m
                    before = carry[i, at[0], at[1]]
                    if m == 0:
                        total[i, at[0], at[1]] = before - fd[c][0]
                        carry[i, at[0], at[1]] = fd[c][0]
                    else:
                        total[i, at[0], at[1]] = before + (fs[c][m] - fd[c][m])
                        carry[i, at[0], at[1]] = fs[c][m] + fd[c][m]


def next_basis(plane, total, step_ref, shift_ref, w_ref, older_ref, out_ref):
    step, shift = step_ref[plane], shift_ref[plane]
    for c in range(3):
        mm, dm, md, dd = (total[4 * c + m] for m in range(4))
        p = (mm - dm) + pltpu.roll(mm + dm, 1, 0)
        q = (md - dd) + pltpu.roll(md + dd, 1, 0)
        force = (p - q) + pltpu.roll(p + q, 1, 1)
        value = step * force + shift * w_ref[c, plane]
        if older_ref is None:
            value = 0.5 * value
        else:
            value = value - older_ref[c, plane]
        out_ref[c, plane] = value


def coefficients(nu):
    half = 0.5

    def gram(i, j):
        return half * (nu[i + j] + nu[abs(i - j)])

    def image(p):
        out = [None] * (len(p) + 1)

        def add(i, value):
            out[i] = value if out[i] is None else out[i] + value

        for k, value in enumerate(p):
            whole, part = SIGMA * value, (0.5 * SIGMA) * value
            add(k, whole)
            if k == 0:
                add(1, whole)
            else:
                add(k + 1, part)
                add(k - 1, part)
        return out

    def form(u, v):
        total = None
        for i, ui in enumerate(u):
            row = None
            for j, vj in enumerate(v):
                term = gram(i, j) * vj
                row = term if row is None else row + term
            total = ui * row if total is None else total + ui * row
        return total

    one = jnp.ones_like(nu[0])
    solution, residual, direction = [], [one], [one]
    descent = gram(0, 0)
    for iteration in range(ITERS):
        moved = image(direction)
        step = descent / form(direction, moved)
        solution = [
            step * p + (solution[k] if k < len(solution) else 0.0) for k, p in enumerate(direction)
        ]
        residual = [
            (residual[k] - step * m) if k < len(residual) else -(step * m)
            for k, m in enumerate(moved)
        ]
        if iteration + 1 < ITERS:
            new = form(residual, residual)
            ratio = new / descent
            direction = [
                r + ratio * direction[k] if k < len(direction) else r
                for k, r in enumerate(residual)
            ]
            descent = new
    return solution, residual


def place(x, y, z, core):
    return {"gx": ((y // 2) * 4 + x) * 2 + core, "gy": lax.rem(y, 2) * 8 + z}


def kernel(r_hbm, l_hbm, sol_ref, res_ref, r_in, labels, diag, step_ref, shift_ref,
           w0, w1, w2, w3, w4, even, odd, carry, total,
           from_x, from_y, from_xy, mine, theirs,
           load_sem, send_sem, recv_sem, edge_send, edge_recv, sum_send, sum_recv):
    gx, gy = lax.axis_index("gx"), lax.axis_index("gy")
    core, x, y_hi = lax.rem(gx, 2), lax.rem(gx // 2, 4), gx // 8
    z, y_lo = lax.rem(gy, 8), gy // 8
    y = y_hi * 2 + y_lo

    own = (pl.ds(HALO, NX), pl.ds(0, NY))
    load_r = pltpu.make_async_copy(r_hbm, r_in.at[:, own[0], own[1]], load_sem.at[0])
    load_l = pltpu.make_async_copy(l_hbm, labels.at[own[0], own[1]], load_sem.at[1])
    load_r.start()
    load_l.start()

    def neighbour(dx, dy):
        return {"gx": lax.rem(gx + dx + GROUP, GROUP), "gy": lax.rem(gy + dy + GROUP, GROUP)}

    stages = [
        [place(lax.rem(x + k // 4, 4), lax.rem(y + k % 4, 4), z, core) for k in range(1, GROUP)],
        [place(x, y, lax.rem(z + k // 2, 8), lax.rem(core + k % 2, 2)) for k in range(1, GROUP)],
    ]
    barrier = pltpu.get_barrier_semaphore()
    greeted = [neighbour(dx, dy) for dx, dy in DIRECTIONS] + stages[0] + stages[1]
    for device in greeted:
        pl.semaphore_signal(barrier, inc=1, device_id=device, device_id_type=MESH)
    carry[...] = jnp.zeros_like(carry)
    load_r.wait()
    load_l.wait()
    pl.semaphore_wait(barrier, len(greeted))

    copies = []
    for number, (dx, dy) in enumerate(DIRECTIONS):
        xs = pl.ds({1: NX, 0: HALO, -1: HALO}[dx], NX if dx == 0 else HALO)
        xd = pl.ds({1: 0, 0: HALO, -1: HALO + NX}[dx], NX if dx == 0 else HALO)
        ys = pl.ds({1: 4, 0: 0, -1: 0}[dy], NY if dy == 0 else HALO)
        yd = pl.ds({1: 12, 0: 0, -1: 8}[dy], NY if dy == 0 else HALO)
        for kind, (source, target) in enumerate((
            (labels.at[xs, ys], labels.at[xd, yd]),
            (r_in.at[:, xs, ys], r_in.at[:, xd, yd]),
        )):
            copy = pltpu.make_async_remote_copy(
                src_ref=source, dst_ref=target,
                send_sem=send_sem.at[kind, number], recv_sem=recv_sem.at[kind, number],
                device_id=neighbour(dx, dy), device_id_type=MESH,
            )
            copy.start()
            copies.append(copy)
    for copy in copies:
        copy.wait()

    def corner_sums(plane):
        value = pick(labels[plane] > 0, lambda la, mu: (la + 4.0 * mu) / 9.0)
        value = value + pltpu.roll(value, 1, 1)
        return value + pltpu.roll(value, 1, 0)

    def diagonal_plane(plane, below):
        here = corner_sums(plane)
        value = here + below + KAPPA
        inverse = 1.0 / value
        diag[plane] = value
        step = STEP * inverse
        step_ref[plane] = step
        shift_ref[plane] = (RAW * KAPPA) * step - 2.0
        for c in range(3):
            w0[c, plane] = r_in[c, plane] * inverse
        return here

    lax.fori_loop(1, PX, diagonal_plane, corner_sums(0))

    def apply(first, last, w_ref, older_ref, out_ref):
        plane_modes(w_ref, first, even)

        def one(plane, lower, upper):
            plane_modes(w_ref, plane + 1, upper)
            voxel_forces(plane, labels, lower, upper, carry, total)
            next_basis(plane, total, step_ref, shift_ref, w_ref, older_ref, out_ref)

        def two(number, _):
            plane = first + 2 * number
            one(plane, even, odd)
            one(plane + 1, odd, even)
            return 0

        count = last - first + 1
        lax.fori_loop(0, count // 2, two, 0)
        if count % 2:
            one(last, even, odd)

    apply(1, 22, w0, None, w1)
    apply(2, 21, w1, w0, w2)
    apply(3, 20, w2, w1, w3)

    edges = [
        (w3.at[:, pl.ds(HALO + NX - 1, 1)], from_x, (1, 0)),
        (w3.at[:, pl.ds(HALO, NX + 1), pl.ds(NY - 1, 1)], from_y.at[:, :, pl.ds(NY - 1, 1)], (0, 1)),
        (w3.at[:, pl.ds(HALO + NX - 1, 1), pl.ds(0, NY)], from_xy, (1, 1)),
    ]
    copies = []
    for number, (source, target, (dx, dy)) in enumerate(edges):
        copy = pltpu.make_async_remote_copy(
            src_ref=source, dst_ref=target,
            send_sem=edge_send.at[number], recv_sem=edge_recv.at[number],
            device_id=neighbour(dx, dy), device_id_type=MESH,
        )
        copy.start()
        copies.append(copy)
    for copy in copies:
        copy.wait()
    for c in range(3):
        w3[c, HALO - 1, 0:8] = from_x[c, 0, 0:8]
        w3[c, HALO - 1, 8:16] = from_x[c, 0, 8:16]
        w3[c, HALO - 1, 15:16] = from_xy[c, 0, 7:8]
        for plane in range(NX + 1):
            w3[c, HALO + plane, 15:16] = from_y[c, plane, 7:8]
    apply(3, 19, w3, w2, w4)

    basis = (w0, w1, w2, w3, w4)

    def inner(number, sums):
        plane = HALO + number
        sums = list(sums)
        for c in range(3):
            for lane in (0, 128):
                at = (slice(0, NY), slice(lane, lane + 128))
                weight = diag[plane, at[0], at[1]]
                w = [ref[c, plane, at[0], at[1]] for ref in basis]
                scaled = [weight * v for v in w[:4]]
                for i, (j, k) in enumerate(DOTS):
                    sums[i] = sums[i] + scaled[j] * w[k]
        return tuple(sums)

    zero = jnp.zeros((NY, 128), jnp.float32)
    sums = lax.fori_loop(0, NX, inner, (zero,) * len(DOTS))
    lane = lax.broadcasted_iota(jnp.int32, (1, 128), 1)
    row = jnp.zeros((1, 128), jnp.float32)
    for i, value in enumerate(sums):
        value = jnp.sum(jnp.sum(value, axis=0, keepdims=True), axis=1, keepdims=True)
        row = jnp.where(lane == i, value, row)
    for stage, devices in enumerate(stages):
        mine[stage] = row
        copies = []
        for number, device in enumerate(devices):
            copy = pltpu.make_async_remote_copy(
                src_ref=mine.at[stage], dst_ref=theirs.at[stage, number],
                send_sem=sum_send.at[stage, number], recv_sem=sum_recv.at[stage, number],
                device_id=device, device_id_type=MESH,
            )
            copy.start()
            copies.append(copy)
        for copy in copies:
            copy.wait()
        for number in range(len(devices)):
            row = row + theirs[stage, number]
    dots = [
        jnp.sum(jnp.where(lane == i, row, 0.0), axis=1, keepdims=True) for i in range(len(DOTS))
    ]
    nu = [
        value if i < 2 else 2.0 * value - dots[i % 2] for i, value in enumerate(dots)
    ]
    solution, residual = coefficients(nu)
    solution = [jnp.broadcast_to(v, (NY, 128)) for v in solution]
    residual = [jnp.broadcast_to(v, (NY, 128)) for v in residual]

    def combine(number, _):
        plane = HALO + number
        for c in range(3):
            for lane in (0, 128):
                at = (slice(0, NY), slice(lane, lane + 128))
                w = [ref[c, plane, at[0], at[1]] for ref in basis]
                x = solution[0] * w[0]
                r = residual[0] * w[0]
                for k in range(1, 5):
                    if k < 4:
                        x = x + solution[k] * w[k]
                    r = r + residual[k] * w[k]
                sol_ref[c, number, at[0], at[1]] = x
                res_ref[c, number, at[0], at[1]] = diag[plane, at[0], at[1]] * r
        return 0

    lax.fori_loop(0, NX, combine, 0)


def local(right_side, labels):
    shape = (3, NX, NY, NZ)
    vector = pltpu.VMEM((3, PX, PY, NZ), jnp.float32)
    scalar = pltpu.VMEM((PX, PY, NZ), jnp.float32)
    modes = pltpu.VMEM((12, PY, NZ), jnp.float32)
    return pl.pallas_call(
        kernel,
        out_shape=(jax.ShapeDtypeStruct(shape, jnp.float32),) * 2,
        in_specs=[pl.BlockSpec(memory_space=pl.ANY)] * 2,
        out_specs=[pl.BlockSpec(memory_space=pltpu.VMEM)] * 2,
        scratch_shapes=[
            vector, pltpu.VMEM((PX, PY, NZ), jnp.int32), scalar, scalar, scalar,
            vector, vector, vector, vector, vector, modes, modes, modes, modes,
            pltpu.VMEM((3, 1, PY, NZ), jnp.float32),
            pltpu.VMEM((3, NX + 1, NY, NZ), jnp.float32),
            pltpu.VMEM((3, 1, NY, NZ), jnp.float32),
            pltpu.VMEM((2, 1, 128), jnp.float32),
            pltpu.VMEM((2, GROUP - 1, 1, 128), jnp.float32),
            pltpu.SemaphoreType.DMA((2,)),
            pltpu.SemaphoreType.DMA((2, 8)),
            pltpu.SemaphoreType.DMA((2, 8)),
            pltpu.SemaphoreType.DMA((3,)),
            pltpu.SemaphoreType.DMA((3,)),
            pltpu.SemaphoreType.DMA((2, GROUP - 1)),
            pltpu.SemaphoreType.DMA((2, GROUP - 1)),
        ],
        compiler_params=pltpu.CompilerParams(
            collective_id=0, has_side_effects=True, vmem_limit_bytes=40 * 1024 * 1024
        ),
    )(right_side, labels)


def solution(mesh):
    specs = P(None, "gx", "gy", None)
    return jax.shard_map(
        local, mesh=mesh, in_specs=(specs, P("gx", "gy", None)), out_specs=(specs, specs),
        check_vma=False,
    )
```

profile of v0, /device:TPU:1, one launch (start us, length us, event | category | flops | bytes accessed | tf_op | source)
XLA Modules:
  0.0 58.6 jit_solution(2834646390911089156)
XLA Ops:
  0.6 0.0 copy-start
  0.6 1.0 %copy-done = f32[3,16,8,256]{3,2,1,0:T(8,128)S(1)} copy-done((f32[3,16,8,256]{3,2,1,0:T(8,128)S(1)}, f32[3,16,8,256]{3,2,1,0:T(8,128)}, u32[]{:S(2)}) %copy-start) | copy-done | bytes 393240
  1.6 0.0 copy-start.1
  1.6 0.9 %copy-done.1 = s32[16,8,256]{2,1,0:T(8,128)S(1)} copy-done((s32[16,8,256]{2,1,0:T(8,128)S(1)}, s32[16,8,256]{2,1,0:T(8,128)}, u32[]{:S(2)}) %copy-start.1) | copy-done | bytes 131096
  2.5 54.5 %shard_map.41 = (f32[3,16,8,256]{3,2,1,0:T(8,128)S(1)}, f32[3,16,8,256]{3,2,1,0:T(8,128)S(1)}) custom-call(f32[3,16,8,256]{3,2,1,0:T(8,128)S(1)} %copy-done, s32[16,8,256]{2,1,0:T(8,128)S(1)} %copy-done.1), custom_call_target="tpu_custom_call" | custom-call | tf_op jit(solution)/shard_map/pallas_call | solution.py:363
  57.1 0.7 %copy.6 = f32[3,16,8,256]{3,2,1,0:T(8,128)} copy(f32[3,16,8,256]{3,2,1,0:T(8,128)S(1)} %get-tuple-element.4) | data formatting | bytes 786432
  57.8 0.7 %copy.7 = f32[3,16,8,256]{3,2,1,0:T(8,128)} copy(f32[3,16,8,256]{3,2,1,0:T(8,128)S(1)} %get-tuple-element.5) | data formatting | bytes 786432
Async XLA Ops:
  0.6 1.0 %copy-start = (f32[3,16,8,256]{3,2,1,0:T(8,128)S(1)}, f32[3,16,8,256]{3,2,1,0:T(8,128)}, u32[]{:S(2)}) copy-start(f32[3,16,8,256]{3,2,1,0:T(8,128)} %r_hbm.1) | copy-start | bytes 1179652
  1.6 0.9 %copy-start.1 = (s32[16,8,256]{2,1,0:T(8,128)S(1)}, s32[16,8,256]{2,1,0:T(8,128)}, u32[]{:S(2)}) copy-start(s32[16,8,256]{2,1,0:T(8,128)} %l_hbm.1) | copy-start | bytes 393220
where the time goes:
time: 58.7 us; the launch traced here: 58.6 us
  Pallas kernels  54.5 us (93%)
  local copies, waits for them, and re-layouts  3.39 us (6%)
  between operations  0.65 us (1%)
    pallas_call x1, Pallas kernels, local(): pl.pallas_call(kernel, out_shape=(jax.ShapeDtypeStruct(shape, jnp.float32...  54.5 us
    unnamed x6, local copies, waits for them, and re-layouts  3.39 us

commit v1 on v0

--- a/solution.py
+++ b/solution.py
@@ -22,8 +22,8 @@
 RAW = 16.0
 STEP = 2.0 / (RAW * SIGMA)
 
-DIRECTIONS = [(1, 0), (1, 1), (1, -1), (0, 1), (0, -1), (-1, 0), (-1, 1), (-1, -1)]
-DOTS = [(0, 0), (0, 1), (1, 1), (1, 2), (2, 2), (2, 3), (3, 3), (3, 4)]
+DIRECTIONS = [(1, 0), (1, 1), (1, -1), (-1, 0), (-1, 1), (-1, -1), (0, 1), (0, -1)]
+DOTS = [(0, 0), (0, 1), (1, 1), (1, 2), (2, 2), (2, 3), (3, 3)]
 
 
 def phases(form):
@@ -97,6 +97,40 @@
                         carry[i, at[0], at[1]] = fs[c][m] + fd[c][m]
 
 
+def voxel_energy(plane, label_ref, at, lower, upper):
+    stiff = label_ref[plane, at[0], at[1]] > 0
+    lam = pick(stiff, lambda la, mu: la)
+    mu = pick(stiff, lambda la, mu: mu)
+    a = [lower[i, at[0], at[1]] for i in range(12)]
+    b = [upper[i, at[0], at[1]] for i in range(12)]
+    d = [[b[4 * c + m] - a[4 * c + m] for m in range(4)] for c in range(3)]
+    s = [[a[4 * c + m] + b[4 * c + m] if m else None for m in range(4)] for c in range(3)]
+
+    def squares(*values):
+        total = None
+        for v in values:
+            total = v * v if total is None else total + v * v
+        return total
+
+    third, ninth = 1.0 / 3.0, 1.0 / 9.0
+    corners = squares(d[0][3], d[1][3], d[2][3])
+    pairs = ((d[0][1], s[2][3]), (d[0][2], s[1][3]), (d[1][1], d[2][2]))
+    singles = (s[0][3], d[1][2], d[2][1])
+    lam_part = (
+        squares(d[0][0] + s[1][1] + s[2][2])
+        + third * squares(*(p + q for p, q in pairs))
+        + ninth * corners
+    )
+    mu_part = (
+        2.0 * squares(d[0][0], s[1][1], s[2][2])
+        + squares(d[1][0] + s[0][1], d[2][0] + s[0][2], s[2][1] + s[1][2])
+        + squares(*(v for pair in pairs for v in pair))
+        + third * (squares(*singles) + squares(singles[0] + singles[1] + singles[2]))
+        + (4.0 * ninth) * corners
+    )
+    return lam * lam_part + mu * mu_part
+
+
 def next_basis(plane, total, step_ref, shift_ref, w_ref, older_ref, out_ref):
     step, shift = step_ref[plane], shift_ref[plane]
     for c in range(3):
@@ -172,20 +206,15 @@
     return {"gx": ((y // 2) * 4 + x) * 2 + core, "gy": lax.rem(y, 2) * 8 + z}
 
 
-def kernel(r_hbm, l_hbm, sol_ref, res_ref, r_in, labels, diag, step_ref, shift_ref,
-           w0, w1, w2, w3, w4, even, odd, carry, total,
-           from_x, from_y, from_xy, mine, theirs,
-           load_sem, send_sem, recv_sem, edge_send, edge_recv, sum_send, sum_recv):
+def kernel(r_hbm, l_hbm, sol_ref, res_ref, r_in, labels, diag, step_ref, shift_ref, below,
+           w0, w1, w2, w3, w4, *rest):
+    sets, rest = [rest[4 * k : 4 * k + 4] for k in range(3)], rest[12:]
+    (from_x, from_y, from_xy, mine, theirs, load_sem, send_sem, recv_sem,
+     face_send, face_recv, edge_send, edge_recv, sum_send, sum_recv) = rest
     gx, gy = lax.axis_index("gx"), lax.axis_index("gy")
     core, x, y_hi = lax.rem(gx, 2), lax.rem(gx // 2, 4), gx // 8
     z, y_lo = lax.rem(gy, 8), gy // 8
     y = y_hi * 2 + y_lo
-
-    own = (pl.ds(HALO, NX), pl.ds(0, NY))
-    load_r = pltpu.make_async_copy(r_hbm, r_in.at[:, own[0], own[1]], load_sem.at[0])
-    load_l = pltpu.make_async_copy(l_hbm, labels.at[own[0], own[1]], load_sem.at[1])
-    load_r.start()
-    load_l.start()
 
     def neighbour(dx, dy):
         return {"gx": lax.rem(gx + dx + GROUP, GROUP), "gy": lax.rem(gy + dy + GROUP, GROUP)}
@@ -198,39 +227,66 @@
     greeted = [neighbour(dx, dy) for dx, dy in DIRECTIONS] + stages[0] + stages[1]
     for device in greeted:
         pl.semaphore_signal(barrier, inc=1, device_id=device, device_id_type=MESH)
-    carry[...] = jnp.zeros_like(carry)
+    own = (pl.ds(HALO, NX), pl.ds(0, NY))
+    load_r = pltpu.make_async_copy(r_hbm, r_in.at[:, own[0], own[1]], load_sem.at[0])
+    load_l = pltpu.make_async_copy(l_hbm, labels.at[own[0], own[1]], load_sem.at[1])
+    load_r.start()
+    load_l.start()
     load_r.wait()
     load_l.wait()
     pl.semaphore_wait(barrier, len(greeted))
 
-    copies = []
-    for number, (dx, dy) in enumerate(DIRECTIONS):
-        xs = pl.ds({1: NX, 0: HALO, -1: HALO}[dx], NX if dx == 0 else HALO)
-        xd = pl.ds({1: 0, 0: HALO, -1: HALO + NX}[dx], NX if dx == 0 else HALO)
-        ys = pl.ds({1: 4, 0: 0, -1: 0}[dy], NY if dy == 0 else HALO)
-        yd = pl.ds({1: 12, 0: 0, -1: 8}[dy], NY if dy == 0 else HALO)
-        for kind, (source, target) in enumerate((
-            (labels.at[xs, ys], labels.at[xd, yd]),
-            (r_in.at[:, xs, ys], r_in.at[:, xd, yd]),
-        )):
-            copy = pltpu.make_async_remote_copy(
-                src_ref=source, dst_ref=target,
-                send_sem=send_sem.at[kind, number], recv_sem=recv_sem.at[kind, number],
-                device_id=neighbour(dx, dy), device_id_type=MESH,
+    def piece(xs, ys, xd, yd, device, sends, recvs):
+        pairs = ((labels.at[xs, ys], labels.at[xd, yd]), (r_in.at[:, xs, ys], r_in.at[:, xd, yd]))
+        return [
+            pltpu.make_async_remote_copy(
+                src_ref=source, dst_ref=target, send_sem=sends(kind), recv_sem=recvs(kind),
+                device_id=device, device_id_type=MESH,
             )
-            copy.start()
-            copies.append(copy)
-    for copy in copies:
-        copy.wait()
+            for kind, (source, target) in enumerate(pairs)
+        ]
+
+    def rows(dy):
+        return (pl.ds({1: 4, 0: 0, -1: 0}[dy], NY if dy == 0 else 4),
+                pl.ds({1: 12, 0: 0, -1: 8}[dy], NY if dy == 0 else 4))
+
+    def slab(number):
+        dx, dy = DIRECTIONS[number]
+        ys, yd = rows(dy)
+        return piece(
+            pl.ds(NX if dx == 1 else HALO, HALO), ys, pl.ds(0 if dx == 1 else HALO + NX, HALO), yd,
+            neighbour(dx, dy),
+            lambda kind: send_sem.at[kind, number], lambda kind: recv_sem.at[kind, number],
+        )
+
+    def face(part, side):
+        ys, yd = rows(1 - 2 * side)
+        at = pl.ds(HALO * part, HALO)
+        return piece(
+            at, ys, at, yd, neighbour(0, 1 - 2 * side),
+            lambda kind: face_send.at[kind, side, part - 1],
+            lambda kind: face_recv.at[kind, side, part - 1],
+        )
+
+    halo = []
+    for number in (0, 1, 2):
+        halo += slab(number)
+    for part in range(1, 5):
+        halo += face(part, 0) + face(part, 1)
+    for number in (3, 4, 5):
+        halo += slab(number)
+    for copy in halo:
+        copy.start()
 
     def corner_sums(plane):
         value = pick(labels[plane] > 0, lambda la, mu: (la + 4.0 * mu) / 9.0)
         value = value + pltpu.roll(value, 1, 1)
         return value + pltpu.roll(value, 1, 0)
 
-    def diagonal_plane(plane, below):
+    def diagonal_plane(plane):
         here = corner_sums(plane)
-        value = here + below + KAPPA
+        value = here + below[...] + KAPPA
+        below[...] = here
         inverse = 1.0 / value
         diag[plane] = value
         step = STEP * inverse
@@ -238,39 +294,64 @@
         shift_ref[plane] = (RAW * KAPPA) * step - 2.0
         for c in range(3):
             w0[c, plane] = r_in[c, plane] * inverse
-        return here
-
-    lax.fori_loop(1, PX, diagonal_plane, corner_sums(0))
-
-    def apply(first, last, w_ref, older_ref, out_ref):
-        plane_modes(w_ref, first, even)
-
-        def one(plane, lower, upper):
-            plane_modes(w_ref, plane + 1, upper)
-            voxel_forces(plane, labels, lower, upper, carry, total)
-            next_basis(plane, total, step_ref, shift_ref, w_ref, older_ref, out_ref)
-
-        def two(number, _):
-            plane = first + 2 * number
-            one(plane, even, odd)
-            one(plane + 1, odd, even)
-            return 0
-
-        count = last - first + 1
-        lax.fori_loop(0, count // 2, two, 0)
-        if count % 2:
-            one(last, even, odd)
-
-    apply(1, 22, w0, None, w1)
-    apply(2, 21, w1, w0, w2)
-    apply(3, 20, w2, w1, w3)
+
+    basis = (w0, w1, w2, w3, w4)
+
+    def level(k, plane, parity):
+        even, odd, carry, total = sets[k - 1]
+        lower, upper = (even, odd) if parity == 0 else (odd, even)
+        older = basis[k - 2] if k > 1 else None
+        plane_modes(basis[k - 1], plane + 1, upper)
+        voxel_forces(plane, labels, lower, upper, carry, total)
+        next_basis(plane, total, step_ref, shift_ref, basis[k - 1], older, basis[k])
+
+    for number in (0, 1, 2):
+        for copy in slab(number):
+            copy.wait_recv()
+    below[...] = corner_sums(0)
+    for p in range(1, 6):
+        if p == 4:
+            for side in (0, 1):
+                for copy in face(1, side):
+                    copy.wait_recv()
+        diagonal_plane(p)
+        for k in (1, 2, 3):
+            if p == 2 * k - 1:
+                plane_modes(basis[k - 1], k, sets[k - 1][k % 2])
+            elif p >= 2 * k:
+                level(k, p - k, (p - k) % 2)
+
+    def two_planes(number, _):
+        first = 6 + 2 * number
+
+        @pl.when(lax.rem(first, 4) == 0)
+        def _():
+            @pl.when(first < HALO + NX)
+            def _():
+                for side in (0, 1):
+                    for copy in face(first // 4, side):
+                        copy.wait_recv()
+
+            @pl.when(first == HALO + NX)
+            def _():
+                for number in (3, 4, 5):
+                    for copy in slab(number):
+                        copy.wait_recv()
+
+        for extra in (0, 1):
+            diagonal_plane(first + extra)
+            for k in (1, 2, 3):
+                level(k, first + extra - k, (extra - k) % 2)
+        return 0
+
+    lax.fori_loop(0, 9, two_planes, 0)
 
     edges = [
         (w3.at[:, pl.ds(HALO + NX - 1, 1)], from_x, (1, 0)),
         (w3.at[:, pl.ds(HALO, NX + 1), pl.ds(NY - 1, 1)], from_y.at[:, :, pl.ds(NY - 1, 1)], (0, 1)),
         (w3.at[:, pl.ds(HALO + NX - 1, 1), pl.ds(0, NY)], from_xy, (1, 1)),
     ]
-    copies = []
+    edge_copies = []
     for number, (source, target, (dx, dy)) in enumerate(edges):
         copy = pltpu.make_async_remote_copy(
             src_ref=source, dst_ref=target,
@@ -278,8 +359,63 @@
             device_id=neighbour(dx, dy), device_id_type=MESH,
         )
         copy.start()
-        copies.append(copy)
-    for copy in copies:
+        edge_copies.append(copy)
+
+    zero = jnp.zeros((NY, 128), jnp.float32)
+    even, odd, carry, total = sets[0]
+    plane_modes(w3, HALO, even)
+
+    def inner(plane, lower, upper, sums):
+        sums = list(sums)
+        plane_modes(w3, plane + 1, upper)
+        for lane in (0, 128):
+            at = (slice(0, NY), slice(lane, lane + 128))
+            weight = diag[plane, at[0], at[1]]
+            for c in range(3):
+                w = [ref[c, plane, at[0], at[1]] for ref in basis[:4]]
+                scaled = [weight * v for v in w]
+                for i, (j, k) in enumerate(DOTS):
+                    sums[i] = sums[i] + scaled[j] * w[k]
+                sums[7] = sums[7] + (RAW * KAPPA) * (w[3] * w[3])
+            sums[7] = sums[7] + voxel_energy(plane, labels, at, lower, upper)
+        return tuple(sums)
+
+    def inner_two(number, sums):
+        plane = HALO + 2 * number
+        sums = inner(plane, even, odd, sums)
+        return inner(plane + 1, odd, even, sums)
+
+    sums = lax.fori_loop(0, NX // 2, inner_two, (zero,) * 8)
+    lane = lax.broadcasted_iota(jnp.int32, (1, 128), 1)
+    row = jnp.zeros((1, 128), jnp.float32)
+    for i, value in enumerate(sums):
+        value = jnp.sum(jnp.sum(value, axis=0, keepdims=True), axis=1, keepdims=True)
+        row = jnp.where(lane == i, value, row)
+
+    def share(stage, row):
+        mine[stage] = row
+        copies = []
+        for number, device in enumerate(stages[stage]):
+            copy = pltpu.make_async_remote_copy(
+                src_ref=mine.at[stage], dst_ref=theirs.at[stage, number],
+                send_sem=sum_send.at[stage, number], recv_sem=sum_recv.at[stage, number],
+                device_id=device, device_id_type=MESH,
+            )
+            copy.start()
+            copies.append(copy)
+        return copies
+
+    def collect(stage, row, copies):
+        for copy in copies:
+            copy.wait()
+        for number in range(len(copies)):
+            row = row + theirs[stage, number]
+        return row
+
+    copies = share(0, row)
+    for copy in halo:
+        copy.wait_send()
+    for copy in edge_copies:
         copy.wait()
     for c in range(3):
         w3[c, HALO - 1, 0:8] = from_x[c, 0, 0:8]
@@ -287,50 +423,33 @@
         w3[c, HALO - 1, 15:16] = from_xy[c, 0, 7:8]
         for plane in range(NX + 1):
             w3[c, HALO + plane, 15:16] = from_y[c, plane, 7:8]
-    apply(3, 19, w3, w2, w4)
-
-    basis = (w0, w1, w2, w3, w4)
-
-    def inner(number, sums):
-        plane = HALO + number
-        sums = list(sums)
-        for c in range(3):
-            for lane in (0, 128):
-                at = (slice(0, NY), slice(lane, lane + 128))
-                weight = diag[plane, at[0], at[1]]
-                w = [ref[c, plane, at[0], at[1]] for ref in basis]
-                scaled = [weight * v for v in w[:4]]
-                for i, (j, k) in enumerate(DOTS):
-                    sums[i] = sums[i] + scaled[j] * w[k]
-        return tuple(sums)
-
-    zero = jnp.zeros((NY, 128), jnp.float32)
-    sums = lax.fori_loop(0, NX, inner, (zero,) * len(DOTS))
-    lane = lax.broadcasted_iota(jnp.int32, (1, 128), 1)
-    row = jnp.zeros((1, 128), jnp.float32)
-    for i, value in enumerate(sums):
-        value = jnp.sum(jnp.sum(value, axis=0, keepdims=True), axis=1, keepdims=True)
-        row = jnp.where(lane == i, value, row)
-    for stage, devices in enumerate(stages):
-        mine[stage] = row
-        copies = []
-        for number, device in enumerate(devices):
-            copy = pltpu.make_async_remote_copy(
-                src_ref=mine.at[stage], dst_ref=theirs.at[stage, number],
-                send_sem=sum_send.at[stage, number], recv_sem=sum_recv.at[stage, number],
-                device_id=device, device_id_type=MESH,
-            )
-            copy.start()
-            copies.append(copy)
-        for copy in copies:
-            copy.wait()
-        for number in range(len(devices)):
-            row = row + theirs[stage, number]
+    row = collect(0, row, copies)
+    copies = share(1, row)
+
+    def last_level(plane, lower, upper):
+        plane_modes(w3, plane + 1, upper)
+        voxel_forces(plane, labels, lower, upper, carry, total)
+        next_basis(plane, total, step_ref, shift_ref, w3, w2, w4)
+
+    def last_two(number, _):
+        plane = HALO - 1 + 2 * number
+        last_level(plane, even, odd)
+        last_level(plane + 1, odd, even)
+        return 0
+
+    plane_modes(w3, HALO - 1, even)
+    lax.fori_loop(0, NX // 2, last_two, 0)
+    last_level(HALO + NX - 1, even, odd)
+
+    row = collect(1, row, copies)
     dots = [
-        jnp.sum(jnp.where(lane == i, row, 0.0), axis=1, keepdims=True) for i in range(len(DOTS))
+        jnp.sum(jnp.where(lane == i, row, 0.0), axis=1, keepdims=True) for i in range(8)
     ]
+    last = (2.0 / (RAW * SIGMA)) * dots[7] - 2.0 * dots[6] - dots[5]
     nu = [
-        value if i < 2 else 2.0 * value - dots[i % 2] for i, value in enumerate(dots)
+        dots[0], dots[1], 2.0 * dots[2] - dots[0], 2.0 * dots[3] - dots[1],
+        2.0 * dots[4] - dots[0], 2.0 * dots[5] - dots[1], 2.0 * dots[6] - dots[0],
+        2.0 * last - dots[1],
     ]
     solution, residual = coefficients(nu)
     solution = [jnp.broadcast_to(v, (NY, 128)) for v in solution]
@@ -363,19 +482,22 @@
     return pl.pallas_call(
         kernel,
         out_shape=(jax.ShapeDtypeStruct(shape, jnp.float32),) * 2,
-        in_specs=[pl.BlockSpec(memory_space=pl.ANY)] * 2,
+        in_specs=[pl.BlockSpec(memory_space=pltpu.HBM)] * 2,
         out_specs=[pl.BlockSpec(memory_space=pltpu.VMEM)] * 2,
         scratch_shapes=[
             vector, pltpu.VMEM((PX, PY, NZ), jnp.int32), scalar, scalar, scalar,
-            vector, vector, vector, vector, vector, modes, modes, modes, modes,
+            pltpu.VMEM((PY, NZ), jnp.float32),
+            vector, vector, vector, vector, vector, *([modes] * 12),
             pltpu.VMEM((3, 1, PY, NZ), jnp.float32),
             pltpu.VMEM((3, NX + 1, NY, NZ), jnp.float32),
             pltpu.VMEM((3, 1, NY, NZ), jnp.float32),
             pltpu.VMEM((2, 1, 128), jnp.float32),
             pltpu.VMEM((2, GROUP - 1, 1, 128), jnp.float32),
             pltpu.SemaphoreType.DMA((2,)),
-            pltpu.SemaphoreType.DMA((2, 8)),
-            pltpu.SemaphoreType.DMA((2, 8)),
+            pltpu.SemaphoreType.DMA((2, 6)),
+            pltpu.SemaphoreType.DMA((2, 6)),
+            pltpu.SemaphoreType.DMA((2, 2, 4)),
+            pltpu.SemaphoreType.DMA((2, 2, 4)),
             pltpu.SemaphoreType.DMA((3,)),
             pltpu.SemaphoreType.DMA((3,)),
             pltpu.SemaphoreType.DMA((2, GROUP - 1)),

time: 58.7 us -> 44.1 us (0.75)
  Pallas kernels: 54.5 us -> 40 us
    pallas_call x1, Pallas kernels: 54.5 us -> 40 us  [local(): pl.pallas_call(kernel, out_shape=(jax.ShapeDtypeStruct(shape, jnp.float32...]
where the time goes in v1:
time: 44.1 us; the launch traced here: 44 us
  Pallas kernels  40 us (91%)
  local copies, waits for them, and re-layouts  3.39 us (8%)
  between operations  0.65 us (1%)
    pallas_call x1, Pallas kernels, local(): pl.pallas_call(kernel, out_shape=(jax.ShapeDtypeStruct(shape, jnp.float32...  40 us
    unnamed x6, local copies, waits for them, and re-layouts  3.39 us

profile of v1, /device:TPU:1, one launch (start us, length us, event | category | flops | bytes accessed | tf_op | source)
XLA Modules:
  0.0 44.0 jit_solution(4085517821234053641)
XLA Ops:
  0.6 0.0 copy-start
  0.6 1.0 %copy-done = f32[3,16,8,256]{3,2,1,0:T(8,128)S(1)} copy-done((f32[3,16,8,256]{3,2,1,0:T(8,128)S(1)}, f32[3,16,8,256]{3,2,1,0:T(8,128)}, u32[]{:S(2)}) %copy-start) | copy-done | bytes 393240
  1.6 0.0 copy-start.1
  1.6 0.9 %copy-done.1 = s32[16,8,256]{2,1,0:T(8,128)S(1)} copy-done((s32[16,8,256]{2,1,0:T(8,128)S(1)}, s32[16,8,256]{2,1,0:T(8,128)}, u32[]{:S(2)}) %copy-start.1) | copy-done | bytes 131096
  2.5 40.0 %shard_map.41 = (f32[3,16,8,256]{3,2,1,0:T(8,128)S(1)}, f32[3,16,8,256]{3,2,1,0:T(8,128)S(1)}) custom-call(f32[3,16,8,256]{3,2,1,0:T(8,128)S(1)} %copy-done, s32[16,8,256]{2,1,0:T(8,128)S(1)} %copy-done.1), custom_call_target="tpu_custom_call" | custom-call | tf_op jit(solution)/shard_map/pallas_call | solution.py:482
  42.5 0.7 %copy.6 = f32[3,16,8,256]{3,2,1,0:T(8,128)} copy(f32[3,16,8,256]{3,2,1,0:T(8,128)S(1)} %get-tuple-element.4) | data formatting | bytes 786432
  43.3 0.7 %copy.7 = f32[3,16,8,256]{3,2,1,0:T(8,128)} copy(f32[3,16,8,256]{3,2,1,0:T(8,128)S(1)} %get-tuple-element.5) | data formatting | bytes 786432
Async XLA Ops:
  0.6 1.0 %copy-start = (f32[3,16,8,256]{3,2,1,0:T(8,128)S(1)}, f32[3,16,8,256]{3,2,1,0:T(8,128)}, u32[]{:S(2)}) copy-start(f32[3,16,8,256]{3,2,1,0:T(8,128)} %r_hbm.1) | copy-start | bytes 1179652
  1.6 0.9 %copy-start.1 = (s32[16,8,256]{2,1,0:T(8,128)S(1)}, s32[16,8,256]{2,1,0:T(8,128)}, u32[]{:S(2)}) copy-start(s32[16,8,256]{2,1,0:T(8,128)} %l_hbm.1) | copy-start | bytes 393220

commit v2 on v1

--- a/solution.py
+++ b/solution.py
@@ -206,8 +206,8 @@
     return {"gx": ((y // 2) * 4 + x) * 2 + core, "gy": lax.rem(y, 2) * 8 + z}
 
 
-def kernel(r_hbm, l_hbm, sol_ref, res_ref, r_in, labels, diag, step_ref, shift_ref, below,
-           w0, w1, w2, w3, w4, *rest):
+def kernel(r_hbm, l_hbm, w0, w1, w2, w3, w4, diag, factors, r_in, labels, step_ref, shift_ref, below,
+           *rest):
     sets, rest = [rest[4 * k : 4 * k + 4] for k in range(3)], rest[12:]
     (from_x, from_y, from_xy, mine, theirs, load_sem, send_sem, recv_sem,
      face_send, face_recv, edge_send, edge_recv, sum_send, sum_recv) = rest
@@ -452,42 +452,63 @@
         2.0 * last - dots[1],
     ]
     solution, residual = coefficients(nu)
-    solution = [jnp.broadcast_to(v, (NY, 128)) for v in solution]
-    residual = [jnp.broadcast_to(v, (NY, 128)) for v in residual]
-
-    def combine(number, _):
-        plane = HALO + number
-        for c in range(3):
-            for lane in (0, 128):
-                at = (slice(0, NY), slice(lane, lane + 128))
-                w = [ref[c, plane, at[0], at[1]] for ref in basis]
-                x = solution[0] * w[0]
-                r = residual[0] * w[0]
-                for k in range(1, 5):
-                    if k < 4:
-                        x = x + solution[k] * w[k]
-                    r = r + residual[k] * w[k]
-                sol_ref[c, number, at[0], at[1]] = x
-                res_ref[c, number, at[0], at[1]] = diag[plane, at[0], at[1]] * r
-        return 0
-
-    lax.fori_loop(0, NX, combine, 0)
+    for k, value in enumerate(solution + residual):
+        factors[k] = jnp.broadcast_to(value, (NY, 128))
+
+
+PART = 4
+
+
+def combine(w0, w1, w2, w3, w4, diag, factors, sol_hbm, res_hbm, sol, res, sems):
+    basis = (w0, w1, w2, w3, w4)
+    solution = [factors[k] for k in range(4)]
+    residual = [factors[4 + k] for k in range(5)]
+    copies = []
+    for part in range(NX // PART):
+        def one(number, _):
+            plane = HALO + number
+            for c in range(3):
+                for lane in (0, 128):
+                    at = (slice(0, NY), slice(lane, lane + 128))
+                    w = [ref[c, plane, at[0], at[1]] for ref in basis]
+                    x = solution[0] * w[0]
+                    r = residual[0] * w[0]
+                    for k in range(1, 5):
+                        if k < 4:
+                            x = x + solution[k] * w[k]
+                        r = r + residual[k] * w[k]
+                    sol[c, number, at[0], at[1]] = x
+                    res[c, number, at[0], at[1]] = diag[plane, at[0], at[1]] * r
+            return 0
+
+        lax.fori_loop(part * PART, part * PART + PART, one, 0)
+        planes = pl.ds(part * PART, PART)
+        for i, (source, target) in enumerate(((sol, sol_hbm), (res, res_hbm))):
+            copy = pltpu.make_async_copy(source.at[:, planes], target.at[:, planes], sems.at[i, part])
+            copy.start()
+            copies.append(copy)
+    for copy in copies:
+        copy.wait()
 
 
 def local(right_side, labels):
     shape = (3, NX, NY, NZ)
+    wide = jax.ShapeDtypeStruct((3, PX, PY, NZ), jnp.float32)
     vector = pltpu.VMEM((3, PX, PY, NZ), jnp.float32)
+    in_vmem = pl.BlockSpec(memory_space=pltpu.VMEM)
+    in_hbm = pl.BlockSpec(memory_space=pltpu.HBM)
     scalar = pltpu.VMEM((PX, PY, NZ), jnp.float32)
     modes = pltpu.VMEM((12, PY, NZ), jnp.float32)
-    return pl.pallas_call(
+    parts = pl.pallas_call(
         kernel,
-        out_shape=(jax.ShapeDtypeStruct(shape, jnp.float32),) * 2,
-        in_specs=[pl.BlockSpec(memory_space=pltpu.HBM)] * 2,
-        out_specs=[pl.BlockSpec(memory_space=pltpu.VMEM)] * 2,
+        out_shape=(*([wide] * 5), jax.ShapeDtypeStruct((PX, PY, NZ), jnp.float32),
+                   jax.ShapeDtypeStruct((9, NY, 128), jnp.float32)),
+        in_specs=[in_hbm] * 2,
+        out_specs=[in_vmem] * 7,
         scratch_shapes=[
-            vector, pltpu.VMEM((PX, PY, NZ), jnp.int32), scalar, scalar, scalar,
+            vector, pltpu.VMEM((PX, PY, NZ), jnp.int32), scalar, scalar,
             pltpu.VMEM((PY, NZ), jnp.float32),
-            vector, vector, vector, vector, vector, *([modes] * 12),
+            *([modes] * 12),
             pltpu.VMEM((3, 1, PY, NZ), jnp.float32),
             pltpu.VMEM((3, NX + 1, NY, NZ), jnp.float32),
             pltpu.VMEM((3, 1, NY, NZ), jnp.float32),
@@ -504,9 +525,18 @@
             pltpu.SemaphoreType.DMA((2, GROUP - 1)),
         ],
         compiler_params=pltpu.CompilerParams(
-            collective_id=0, has_side_effects=True, vmem_limit_bytes=40 * 1024 * 1024
+            collective_id=0, has_side_effects=True, vmem_limit_bytes=24 * 1024 * 1024
         ),
-    )(right_side, labels)
+    )(*(pltpu.with_memory_space_constraint(a, pltpu.HBM) for a in (right_side, labels)))
+    block = pltpu.VMEM(shape, jnp.float32)
+    return pl.pallas_call(
+        combine,
+        out_shape=(jax.ShapeDtypeStruct(shape, jnp.float32),) * 2,
+        in_specs=[in_vmem] * 7,
+        out_specs=[in_hbm] * 2,
+        scratch_shapes=[block, block, pltpu.SemaphoreType.DMA((2, NX // PART))],
+        compiler_params=pltpu.CompilerParams(vmem_limit_bytes=8 * 1024 * 1024),
+    )(*parts)
 
 
 def solution(mesh):

time: 44.1 us -> 41.8 us (0.948)
  local copies, waits for them, and re-layouts: 3.39 us -> 0 us
  Pallas kernels: 40 us -> 41.1 us
    unnamed x6 -> x0, local copies, waits for them, and re-layouts: 3.39 us -> none
    pallas_call x1 -> x2, Pallas kernels: 40 us -> 41.1 us  [the longest x1 40 us: local(): pl.pallas_call(kernel, out_shape=(*[wide] * 5, jax.ShapeDtypeStruct((PX,...]
where the time goes in v2:
time: 41.8 us; the launch traced here: 41.7 us
  Pallas kernels  41.1 us (98%)
  between operations  0.64 us (2%)
    pallas_call x1, Pallas kernels, local(): pl.pallas_call(kernel, out_shape=(*[wide] * 5, jax.ShapeDtypeStruct((PX,...  40 us
    pallas_call x1, Pallas kernels, local(): pl.pallas_call(combine, out_shape=(jax.ShapeDtypeStruct(shape, jnp.float3...  1.07 us

profile of v2, /device:TPU:1, one launch (start us, length us, event | category | flops | bytes accessed | tf_op | source)
XLA Modules:
  0.0 41.7 jit_solution(17396752654684304656)
XLA Ops:
  0.6 40.0 %shard_map.41 = (f32[3,24,16,256]{3,2,1,0:T(8,128)S(1)}, f32[3,24,16,256]{3,2,1,0:T(8,128)S(1)}, f32[3,24,16,256]{3,2,1,0:T(8,128)S(1)}, f32[3,24,16,256]{3,2,1,...) custom-call(f32[3,16,8,256]{3,2,1,0:T(8,128)} %r_hbm.1, ...), custom_call_target="tpu_custom_call" | custom-call | tf_op jit(solution)/shard_map/pallas_call | solution.py:502
  40.7 1.1 %shard_map.42 = (f32[3,16,8,256]{3,2,1,0:T(8,128)}, f32[3,16,8,256]{3,2,1,0:T(8,128)}) custom-call(f32[3,24,16,256]{3,2,1,0:T(8,128)S(1)} %get-tuple-element.9.w0, f32[3,24,16,256]{3,2,1,0:T(8,128)S(1)} %get-tuple-element.10.w1, f32[3,24,16,256]{3,2,1,0:T(8,128)S(1)} %get-tuple-element.11.w2, f32[3,24,16,256]{3,2,1,0:T(8,128)S(1)} %get-tuple-element.12.w3, ...), custom_call_target="tpu_custom_call" | custom-call | tf_op jit(solution)/shard_map/pallas_call | solution.py:532

commit v3 on v2

--- a/solution.py
+++ b/solution.py
@@ -37,64 +37,97 @@
     return jnp.where(stiff_mask, jnp.float32(stiff), jnp.float32(soft))
 
 
-def plane_modes(w_ref, plane, modes):
+TILES = ((0, 0), (0, 1), (1, 0), (1, 1))
+
+
+def tile(t):
+    row, half = t
+    return slice(8 * row, 8 * row + 8), slice(128 * half, 128 * half + 128)
+
+
+def along_z(pair, shift):
+    edge = 127 if shift < 0 else 0
+    at_edge = lax.broadcasted_iota(jnp.int32, (8, 128), 1) == edge
+    low, high = (pltpu.roll(v, shift % 128, 1) for v in pair)
+    return jnp.where(at_edge, high, low), jnp.where(at_edge, low, high)
+
+
+def along_y(pair, shift):
+    edge = 7 if shift < 0 else 0
+    at_edge = lax.broadcasted_iota(jnp.int32, (8, 128), 0) == edge
+    low, high = (pltpu.roll(v, shift % 8, 0) for v in pair)
+    return jnp.where(at_edge, high, low), jnp.where(at_edge, low, high)
+
+
+def plane_modes(w_ref, plane, modes, tiles=TILES):
     for c in range(3):
-        u = w_ref[c, plane]
-        uz = pltpu.roll(u, NZ - 1, 1)
-        s, d = u + uz, uz - u
-        sy, dy = pltpu.roll(s, PY - 1, 0), pltpu.roll(d, PY - 1, 0)
-        modes[4 * c] = s + sy
-        modes[4 * c + 1] = sy - s
-        modes[4 * c + 2] = d + dy
-        modes[4 * c + 3] = dy - d
-
-
-def voxel_forces(plane, label_ref, lower, upper, carry, total):
-    for row in (0, 8):
-        for lane in (0, 128):
-            at = (slice(row, row + 8), slice(lane, lane + 128))
-            stiff = label_ref[plane, at[0], at[1]] > 0
-            lam = pick(stiff, lambda la, mu: la)
-            mu = pick(stiff, lambda la, mu: mu)
-            mu2 = pick(stiff, lambda la, mu: 2.0 * mu)
-            lam3 = pick(stiff, lambda la, mu: la / 3.0)
-            mu3 = pick(stiff, lambda la, mu: mu / 3.0)
-            dd9 = pick(stiff, lambda la, mu: (la + 4.0 * mu) / 9.0)
-            a = [lower[i, at[0], at[1]] for i in range(12)]
-            b = [upper[i, at[0], at[1]] for i in range(12)]
-            d = [[b[4 * c + m] - a[4 * c + m] for m in range(4)] for c in range(3)]
-            s = [[a[4 * c + m] + b[4 * c + m] if m else None for m in range(4)] for c in range(3)]
-            fd = [[None] * 4 for _ in range(3)]
-            fs = [[None] * 4 for _ in range(3)]
-            trace = lam * (d[0][0] + s[1][1] + s[2][2])
-            fd[0][0] = trace + mu2 * d[0][0]
-            fs[1][1] = trace + mu2 * s[1][1]
-            fs[2][2] = trace + mu2 * s[2][2]
-            fd[1][0] = fs[0][1] = mu * (d[1][0] + s[0][1])
-            fd[2][0] = fs[0][2] = mu * (d[2][0] + s[0][2])
-            fs[2][1] = fs[1][2] = mu * (s[2][1] + s[1][2])
-            h = lam3 * (d[0][1] + s[2][3])
-            fd[0][1], fs[2][3] = h + mu * d[0][1], h + mu * s[2][3]
-            h = lam3 * (d[0][2] + s[1][3])
-            fd[0][2], fs[1][3] = h + mu * d[0][2], h + mu * s[1][3]
-            h = lam3 * (d[1][1] + d[2][2])
-            fd[1][1], fd[2][2] = h + mu * d[1][1], h + mu * d[2][2]
-            three = s[0][3] + d[1][2] + d[2][1]
-            fs[0][3] = mu3 * (s[0][3] + three)
-            fd[1][2] = mu3 * (d[1][2] + three)
-            fd[2][1] = mu3 * (d[2][1] + three)
-            for c in range(3):
-                fd[c][3] = dd9 * d[c][3]
-            for c in range(3):
-                for m in range(4):
-                    i = 4 * c + m
-                    before = carry[i, at[0], at[1]]
-                    if m == 0:
-                        total[i, at[0], at[1]] = before - fd[c][0]
-                        carry[i, at[0], at[1]] = fd[c][0]
-                    else:
-                        total[i, at[0], at[1]] = before + (fs[c][m] - fd[c][m])
-                        carry[i, at[0], at[1]] = fs[c][m] + fd[c][m]
+        flat = {}
+        for row in (0, 1):
+            u = [w_ref[(c, plane, *tile((row, half)))] for half in (0, 1)]
+            uz = along_z(u, -1)
+            for half in (0, 1):
+                flat[row, half] = (u[half] + uz[half], uz[half] - u[half])
+        for kind in (0, 1):
+            for half in (0, 1):
+                value = [flat[row, half][kind] for row in (0, 1)]
+                above = along_y(value, -1)
+                for row in (0, 1):
+                    if (row, half) in tiles:
+                        at = tile((row, half))
+                        modes[4 * c + 2 * kind, at[0], at[1]] = value[row] + above[row]
+                        modes[4 * c + 2 * kind + 1, at[0], at[1]] = above[row] - value[row]
+
+
+def voxel_forces(plane, label_ref, lower, upper, carry, level):
+    for row, half in TILES:
+        at = tile((row, half))
+        stiff = label_ref[plane, at[0], at[1]] > 0
+        lam = pick(stiff, lambda la, mu: la)
+        mu = pick(stiff, lambda la, mu: mu)
+        mu2 = pick(stiff, lambda la, mu: 2.0 * mu)
+        lam3 = pick(stiff, lambda la, mu: la / 3.0)
+        mu3 = pick(stiff, lambda la, mu: mu / 3.0)
+        dd9 = pick(stiff, lambda la, mu: (la + 4.0 * mu) / 9.0)
+        a = [lower[i, at[0], at[1]] for i in range(12)]
+        b = [upper[i, at[0], at[1]] for i in range(12)]
+        d = [[b[4 * c + m] - a[4 * c + m] for m in range(4)] for c in range(3)]
+        s = [[a[4 * c + m] + b[4 * c + m] if m else None for m in range(4)] for c in range(3)]
+        fd = [[None] * 4 for _ in range(3)]
+        fs = [[None] * 4 for _ in range(3)]
+        trace = lam * (d[0][0] + s[1][1] + s[2][2])
+        fd[0][0] = trace + mu2 * d[0][0]
+        fs[1][1] = trace + mu2 * s[1][1]
+        fs[2][2] = trace + mu2 * s[2][2]
+        fd[1][0] = fs[0][1] = mu * (d[1][0] + s[0][1])
+        fd[2][0] = fs[0][2] = mu * (d[2][0] + s[0][2])
+        fs[2][1] = fs[1][2] = mu * (s[2][1] + s[1][2])
+        h = lam3 * (d[0][1] + s[2][3])
+        fd[0][1], fs[2][3] = h + mu * d[0][1], h + mu * s[2][3]
+        h = lam3 * (d[0][2] + s[1][3])
+        fd[0][2], fs[1][3] = h + mu * d[0][2], h + mu * s[1][3]
+        h = lam3 * (d[1][1] + d[2][2])
+        fd[1][1], fd[2][2] = h + mu * d[1][1], h + mu * d[2][2]
+        three = s[0][3] + d[1][2] + d[2][1]
+        fs[0][3] = mu3 * (s[0][3] + three)
+        fd[1][2] = mu3 * (d[1][2] + three)
+        fd[2][1] = mu3 * (d[2][1] + three)
+        for c in range(3):
+            fd[c][3] = dd9 * d[c][3]
+        for c in range(3):
+            node = []
+            for m in range(4):
+                i = 4 * c + m
+                before = carry[i, at[0], at[1]]
+                if m == 0:
+                    node.append(before - fd[c][0])
+                    carry[i, at[0], at[1]] = fd[c][0]
+                else:
+                    node.append(before + (fs[c][m] - fd[c][m]))
+                    carry[i, at[0], at[1]] = fs[c][m] + fd[c][m]
+            for kind in (0, 1):
+                m, d_ = node[2 * kind], node[2 * kind + 1]
+                level[2 * c + kind, at[0], at[1]] = m - d_
+                level[6 + 2 * c + kind, at[0], at[1]] = m + d_
 
 
 def voxel_energy(plane, label_ref, at, lower, upper):
@@ -131,19 +164,26 @@
     return lam * lam_part + mu * mu_part
 
 
-def next_basis(plane, total, step_ref, shift_ref, w_ref, older_ref, out_ref):
-    step, shift = step_ref[plane], shift_ref[plane]
+def next_basis(plane, level, step_ref, shift_ref, w_ref, older_ref, out_ref, rows=(0, 1)):
     for c in range(3):
-        mm, dm, md, dd = (total[4 * c + m] for m in range(4))
-        p = (mm - dm) + pltpu.roll(mm + dm, 1, 0)
-        q = (md - dd) + pltpu.roll(md + dd, 1, 0)
-        force = (p - q) + pltpu.roll(p + q, 1, 1)
-        value = step * force + shift * w_ref[c, plane]
-        if older_ref is None:
-            value = 0.5 * value
-        else:
-            value = value - older_ref[c, plane]
-        out_ref[c, plane] = value
+        sums = {}
+        for half in (0, 1):
+            for kind in (0, 1):
+                at = [tile((row, half)) for row in (0, 1)]
+                moved = along_y([level[(6 + 2 * c + kind, *at[row])] for row in (0, 1)], 1)
+                for row in rows:
+                    sums[row, half, kind] = level[(2 * c + kind, *at[row])] + moved[row]
+        for row in rows:
+            upper = along_z([sums[row, half, 0] + sums[row, half, 1] for half in (0, 1)], 1)
+            for half in (0, 1):
+                at = tile((row, half))
+                force = (sums[row, half, 0] - sums[row, half, 1]) + upper[half]
+                value = step_ref[(plane, *at)] * force + shift_ref[(plane, *at)] * w_ref[(c, plane, *at)]
+                if older_ref is None:
+                    value = 0.5 * value
+                else:
+                    value = value - older_ref[(c, plane, *at)]
+                out_ref[(c, plane, *at)] = value
 
 
 def coefficients(nu):
@@ -208,7 +248,7 @@
 
 def kernel(r_hbm, l_hbm, w0, w1, w2, w3, w4, diag, factors, r_in, labels, step_ref, shift_ref, below,
            *rest):
-    sets, rest = [rest[4 * k : 4 * k + 4] for k in range(3)], rest[12:]
+    sets, rest = [rest[5 * k : 5 * k + 5] for k in range(3)], rest[15:]
     (from_x, from_y, from_xy, mine, theirs, load_sem, send_sem, recv_sem,
      face_send, face_recv, edge_send, edge_recv, sum_send, sum_recv) = rest
     gx, gy = lax.axis_index("gx"), lax.axis_index("gy")
@@ -261,7 +301,7 @@
 
     def face(part, side):
         ys, yd = rows(1 - 2 * side)
-        at = pl.ds(HALO * part, HALO)
+        at = pl.ds(2 * part + 2, 2)
         return piece(
             at, ys, at, yd, neighbour(0, 1 - 2 * side),
             lambda kind: face_send.at[kind, side, part - 1],
@@ -271,7 +311,7 @@
     halo = []
     for number in (0, 1, 2):
         halo += slab(number)
-    for part in range(1, 5):
+    for part in range(1, 9):
         halo += face(part, 0) + face(part, 1)
     for number in (3, 4, 5):
         halo += slab(number)
@@ -297,54 +337,79 @@
 
     basis = (w0, w1, w2, w3, w4)
 
-    def level(k, plane, parity):
-        even, odd, carry, total = sets[k - 1]
-        lower, upper = (even, odd) if parity == 0 else (odd, even)
-        older = basis[k - 2] if k > 1 else None
-        plane_modes(basis[k - 1], plane + 1, upper)
-        voxel_forces(plane, labels, lower, upper, carry, total)
-        next_basis(plane, total, step_ref, shift_ref, basis[k - 1], older, basis[k])
-
-    for number in (0, 1, 2):
-        for copy in slab(number):
+    def modes_of(k, plane, parity, tiles=TILES, ref=None):
+        ref = basis[k - 1] if ref is None else ref
+        plane_modes(ref, plane, sets[k - 1][parity], tiles)
+
+    def forces_of(k, plane, parity):
+        group = sets[k - 1]
+        voxel_forces(plane, labels, group[parity], group[1 - parity], group[4],
+                     group[2 + parity])
+
+    def next_of(k, plane, parity):
+        group, older = sets[k - 1], basis[k - 2] if k > 1 else None
+        next_basis(plane, group[2 + parity], step_ref, shift_ref,
+                   basis[k - 1], older, basis[k])
+
+    def level(k, plane, parity, count):
+        for i in range(count):
+            modes_of(k, plane + i + 1, (parity + i + 1) % 2)
+            forces_of(k, plane + i, (parity + i) % 2)
+        for i in range(count):
+            next_of(k, plane + i, (parity + i) % 2)
+
+    def arrived(copies):
+        for copy in copies:
             copy.wait_recv()
-    below[...] = corner_sums(0)
-    for p in range(1, 6):
-        if p == 4:
-            for side in (0, 1):
-                for copy in face(1, side):
-                    copy.wait_recv()
-        diagonal_plane(p)
-        for k in (1, 2, 3):
-            if p == 2 * k - 1:
-                plane_modes(basis[k - 1], k, sets[k - 1][k % 2])
-            elif p >= 2 * k:
-                level(k, p - k, (p - k) % 2)
-
-    def two_planes(number, _):
-        first = 6 + 2 * number
-
-        @pl.when(lax.rem(first, 4) == 0)
-        def _():
-            @pl.when(first < HALO + NX)
-            def _():
-                for side in (0, 1):
-                    for copy in face(first // 4, side):
-                        copy.wait_recv()
-
-            @pl.when(first == HALO + NX)
-            def _():
-                for number in (3, 4, 5):
-                    for copy in slab(number):
-                        copy.wait_recv()
-
+
+    def levels(first, which):
+        for k in which:
+            level(k, first - 3 * k, k % 2, 2)
+
+    def diagonals(first):
         for extra in (0, 1):
             diagonal_plane(first + extra)
-            for k in (1, 2, 3):
-                level(k, first + extra - k, (extra - k) % 2)
+
+    below[...] = jnp.zeros_like(below)
+    arrived(slab(0) + slab(1) + slab(2))
+    diagonals(0)
+    diagonals(2)
+    modes_of(1, 1, 1)
+    levels(4, (1,))
+    arrived(face(1, 0) + face(1, 1))
+    diagonals(4)
+    modes_of(2, 2, 0)
+    levels(6, (1,))
+    arrived(face(2, 0) + face(2, 1))
+    diagonals(6)
+    levels(8, (2, 1))
+    arrived(face(3, 0) + face(3, 1))
+    diagonals(8)
+    modes_of(3, 3, 1)
+    levels(10, (2, 1))
+    arrived(face(4, 0) + face(4, 1))
+    diagonals(10)
+
+    def steady(number, _):
+        first = 12 + 2 * number
+
+        @pl.when(first < HALO + NX)
+        def _():
+            part = first // 2 - 1
+            arrived(face(part, 0) + face(part, 1))
+
+        @pl.when(first == HALO + NX)
+        def _():
+            arrived(slab(3) + slab(4) + slab(5))
+
+        levels(first, (3, 2, 1))
+        diagonals(first)
         return 0
 
-    lax.fori_loop(0, 9, two_planes, 0)
+    lax.fori_loop(0, 6, steady, 0)
+    levels(24, (3, 2, 1))
+    levels(26, (3, 2))
+    levels(28, (3,))
 
     edges = [
         (w3.at[:, pl.ds(HALO + NX - 1, 1)], from_x, (1, 0)),
@@ -362,12 +427,13 @@
         edge_copies.append(copy)
 
     zero = jnp.zeros((NY, 128), jnp.float32)
-    even, odd, carry, total = sets[0]
-    plane_modes(w3, HALO, even)
-
-    def inner(plane, lower, upper, sums):
+    near = TILES[:2]
+    modes_of(1, HALO, 0, near, w3)
+
+    def inner(plane, parity, sums):
         sums = list(sums)
-        plane_modes(w3, plane + 1, upper)
+        modes_of(1, plane + 1, 1 - parity, near, w3)
+        lower, upper = sets[0][parity], sets[0][1 - parity]
         for lane in (0, 128):
             at = (slice(0, NY), slice(lane, lane + 128))
             weight = diag[plane, at[0], at[1]]
@@ -382,8 +448,8 @@
 
     def inner_two(number, sums):
         plane = HALO + 2 * number
-        sums = inner(plane, even, odd, sums)
-        return inner(plane + 1, odd, even, sums)
+        sums = inner(plane, 0, sums)
+        return inner(plane + 1, 1, sums)
 
     sums = lax.fori_loop(0, NX // 2, inner_two, (zero,) * 8)
     lane = lax.broadcasted_iota(jnp.int32, (1, 128), 1)
@@ -426,20 +492,21 @@
     row = collect(0, row, copies)
     copies = share(1, row)
 
-    def last_level(plane, lower, upper):
-        plane_modes(w3, plane + 1, upper)
-        voxel_forces(plane, labels, lower, upper, carry, total)
-        next_basis(plane, total, step_ref, shift_ref, w3, w2, w4)
+    def last_level(plane, parity):
+        modes_of(1, plane + 1, 1 - parity, TILES, w3)
+        forces_of(1, plane, parity)
+        next_basis(plane, sets[0][2 + parity], step_ref, shift_ref,
+                   w3, w2, w4, (0,))
 
     def last_two(number, _):
         plane = HALO - 1 + 2 * number
-        last_level(plane, even, odd)
-        last_level(plane + 1, odd, even)
+        last_level(plane, 1)
+        last_level(plane + 1, 0)
         return 0
 
-    plane_modes(w3, HALO - 1, even)
+    modes_of(1, HALO - 1, 1, TILES, w3)
     lax.fori_loop(0, NX // 2, last_two, 0)
-    last_level(HALO + NX - 1, even, odd)
+    last_level(HALO + NX - 1, 1)
 
     row = collect(1, row, copies)
     dots = [
@@ -508,7 +575,7 @@
         scratch_shapes=[
             vector, pltpu.VMEM((PX, PY, NZ), jnp.int32), scalar, scalar,
             pltpu.VMEM((PY, NZ), jnp.float32),
-            *([modes] * 12),
+            *([modes] * 15),
             pltpu.VMEM((3, 1, PY, NZ), jnp.float32),
             pltpu.VMEM((3, NX + 1, NY, NZ), jnp.float32),
             pltpu.VMEM((3, 1, NY, NZ), jnp.float32),
@@ -517,8 +584,8 @@
             pltpu.SemaphoreType.DMA((2,)),
             pltpu.SemaphoreType.DMA((2, 6)),
             pltpu.SemaphoreType.DMA((2, 6)),
-            pltpu.SemaphoreType.DMA((2, 2, 4)),
-            pltpu.SemaphoreType.DMA((2, 2, 4)),
+            pltpu.SemaphoreType.DMA((2, 2, 8)),
+            pltpu.SemaphoreType.DMA((2, 2, 8)),
             pltpu.SemaphoreType.DMA((3,)),
             pltpu.SemaphoreType.DMA((3,)),
             pltpu.SemaphoreType.DMA((2, GROUP - 1)),

time: 41.8 us -> 41.1 us (0.983)
  Pallas kernels: 41.1 us -> 40.4 us
    pallas_call x1, Pallas kernels: 40 us -> 39.3 us  [local(): pl.pallas_call(kernel, out_shape=(*[wide] * 5, jax.ShapeDtypeStruct((PX,...]
where the time goes in v3:
time: 41.1 us; the launch traced here: 41 us
  Pallas kernels  40.4 us (98%)
  between operations  0.64 us (2%)
    pallas_call x1, Pallas kernels, local(): pl.pallas_call(kernel, out_shape=(*[wide] * 5, jax.ShapeDtypeStruct((PX,...  39.3 us
    pallas_call x1, Pallas kernels, local(): pl.pallas_call(combine, out_shape=(jax.ShapeDtypeStruct(shape, jnp.float3...  1.07 us

profile of v3, /device:TPU:1, one launch (start us, length us, event | category | flops | bytes accessed | tf_op | source)
XLA Modules:
  0.0 41.0 jit_solution(18403264500592437098)
XLA Ops:
  0.6 39.3 %shard_map.41 = (f32[3,24,16,256]{3,2,1,0:T(8,128)S(1)}, f32[3,24,16,256]{3,2,1,0:T(8,128)S(1)}, f32[3,24,16,256]{3,2,1,0:T(8,128)S(1)}, f32[3,24,16,256]{3,2,1,...) custom-call(f32[3,16,8,256]{3,2,1,0:T(8,128)} %r_hbm.1, ...), custom_call_target="tpu_custom_call" | custom-call | tf_op jit(solution)/shard_map/pallas_call | solution.py:569
  40.0 1.1 %shard_map.42 = (f32[3,16,8,256]{3,2,1,0:T(8,128)}, f32[3,16,8,256]{3,2,1,0:T(8,128)}) custom-call(f32[3,24,16,256]{3,2,1,0:T(8,128)S(1)} %get-tuple-element.9.w0, f32[3,24,16,256]{3,2,1,0:T(8,128)S(1)} %get-tuple-element.10.w1, f32[3,24,16,256]{3,2,1,0:T(8,128)S(1)} %get-tuple-element.11.w2, f32[3,24,16,256]{3,2,1,0:T(8,128)S(1)} %get-tuple-element.12.w3, ...), custom_call_target="tpu_custom_call" | custom-call | tf_op jit(solution)/shard_map/pallas_call | solution.py:599

commit v4 on v3

--- a/solution.py
+++ b/solution.py
@@ -260,8 +260,8 @@
         return {"gx": lax.rem(gx + dx + GROUP, GROUP), "gy": lax.rem(gy + dy + GROUP, GROUP)}
 
     stages = [
+        [place(x, y, lax.rem(z + k // 2, 8), lax.rem(core + k % 2, 2)) for k in range(1, GROUP)],
         [place(lax.rem(x + k // 4, 4), lax.rem(y + k % 4, 4), z, core) for k in range(1, GROUP)],
-        [place(x, y, lax.rem(z + k // 2, 8), lax.rem(core + k % 2, 2)) for k in range(1, GROUP)],
     ]
     barrier = pltpu.get_barrier_semaphore()
     greeted = [neighbour(dx, dy) for dx, dy in DIRECTIONS] + stages[0] + stages[1]

time: 41.1 us -> 40.1 us (0.976)
  Pallas kernels: 40.4 us -> 39.3 us
    pallas_call x1, Pallas kernels: 39.3 us -> 38.3 us  [local(): pl.pallas_call(kernel, out_shape=(*[wide] * 5, jax.ShapeDtypeStruct((PX,...]
where the time goes in v4:
time: 40.1 us; the launch traced here: 40 us
  Pallas kernels  39.3 us (98%)
  between operations  0.64 us (2%)
    pallas_call x1, Pallas kernels, local(): pl.pallas_call(kernel, out_shape=(*[wide] * 5, jax.ShapeDtypeStruct((PX,...  38.3 us
    pallas_call x1, Pallas kernels, local(): pl.pallas_call(combine, out_shape=(jax.ShapeDtypeStruct(shape, jnp.float3...  1.07 us

profile of v4, /device:TPU:1, one launch (start us, length us, event | category | flops | bytes accessed | tf_op | source)
XLA Modules:
  0.0 40.0 jit_solution(14872947222186646051)
XLA Ops:
  0.6 38.3 %shard_map.41 = (f32[3,24,16,256]{3,2,1,0:T(8,128)S(1)}, f32[3,24,16,256]{3,2,1,0:T(8,128)S(1)}, f32[3,24,16,256]{3,2,1,0:T(8,128)S(1)}, f32[3,24,16,256]{3,2,1,...) custom-call(f32[3,16,8,256]{3,2,1,0:T(8,128)} %r_hbm.1, ...), custom_call_target="tpu_custom_call" | custom-call | tf_op jit(solution)/shard_map/pallas_call | solution.py:569
  38.9 1.1 %shard_map.42 = (f32[3,16,8,256]{3,2,1,0:T(8,128)}, f32[3,16,8,256]{3,2,1,0:T(8,128)}) custom-call(f32[3,24,16,256]{3,2,1,0:T(8,128)S(1)} %get-tuple-element.9.w0, f32[3,24,16,256]{3,2,1,0:T(8,128)S(1)} %get-tuple-element.10.w1, f32[3,24,16,256]{3,2,1,0:T(8,128)S(1)} %get-tuple-element.11.w2, f32[3,24,16,256]{3,2,1,0:T(8,128)S(1)} %get-tuple-element.12.w3, ...), custom_call_target="tpu_custom_call" | custom-call | tf_op jit(solution)/shard_map/pallas_call | solution.py:599
